TPU v7x, 32 devices: a whole 2x2x4 slice. The times are simulated.
32 devices in a mesh: dp: 8 (over z, x), seq: 4 (over y, core).
Axes of the slice: x: 2, y: 2, z: 4, core: 2. Of those that a mesh axis runs over, the one named last changes fastest.
Arguments:
- hidden: bfloat16 [8, 4096, 4096], P('dp', 'seq'), may hold values from -6 to 6
- value_weight: bfloat16 [4096, 64], replicated, may hold values from -0.09375 to 0.09375
- value_bias: float32 [64], replicated, may hold values from -1 to 1
- returns: float32 [8, 4096], P('dp', 'seq'), may hold values from -12 to 12, as said below
- task_bins: int32 [8, 4096], P('dp', 'seq'), may hold values from 0 to 63
- loss_mask: int32 [8, 4096], P('dp', 'seq'), may hold values 0 or 1
Outputs:
- targets: float32 [8, 4096], P('dp', 'seq')
- weight_grad: float32 [4096, 64], replicated
- bias_grad: float32 [64], replicated
Inputs may be any that keep to these rules, and one draw needn't show every extreme that they name: The returns of one rollout share a level and a trend along positions.
All inputs are finite; a program needn't handle non-finite values.
Results may differ from a plain program's by a relative error of at most 0.00083.
Values sent between devices are 32-bit elements.
No kernel may reach another device: no remote copies, remote signals or barrier semaphores. Data moves between devices by JAX's collectives and lax.ppermute only.
A program may use at most 64 MiB of HBM per device.

v0:
```python
import jax
import jax.numpy as jnp
from jax import lax
from jax.sharding import PartitionSpec as P


def on_device(hidden, value_weight, value_bias, returns, task_bins, loss_mask):
    rollouts = hidden.shape[0] * lax.axis_size("dp")
    states = hidden.reshape(-1, hidden.shape[2])
    flat_returns = returns.reshape(-1)
    bins_iota = jnp.arange(value_weight.shape[1], dtype=jnp.int32)
    chosen = (task_bins.reshape(-1)[:, None] == bins_iota).astype(jnp.float32)
    valid = loss_mask.reshape(-1).astype(jnp.float32)
    onehot = chosen * valid[:, None]
    scores = jnp.dot(states, value_weight, preferred_element_type=jnp.float32)
    counts = jnp.sum(onehot, axis=0)
    summed = jnp.sum(onehot * flat_returns[:, None], axis=0)
    squares = jnp.sum(onehot * flat_returns[:, None] * flat_returns[:, None], axis=0)
    counts, summed, squares = lax.psum((counts, summed, squares), ("dp", "seq"))
    means = summed / jnp.maximum(counts, 1.0)
    second = squares - summed * means
    floor_counts = jnp.maximum(counts, 1.0)
    spread = jnp.sqrt(second / floor_counts + 0.1)
    deviation = flat_returns[:, None] - means
    targets = jnp.sum(chosen * (deviation / spread), axis=-1)
    predicted = jnp.sum((scores + value_bias) * chosen, axis=-1)
    slope = valid * jnp.clip(predicted - targets, -1.0, 1.0) / rollouts
    coefficient = chosen * slope[:, None]
    weight_grad = lax.dot_general(
        states,
        coefficient.astype(jnp.bfloat16),
        (((0,), (0,)), ((), ())),
        preferred_element_type=jnp.float32,
    )
    bias_grad = jnp.sum(coefficient, axis=0)
    weight_grad, bias_grad = lax.psum((weight_grad, bias_grad), ("dp", "seq"))
    return (targets.reshape(returns.shape), weight_grad, bias_grad)


def solution(mesh):
    placed = (P("dp", "seq", None), P(), P(), P("dp", "seq"), P("dp", "seq"), P("dp", "seq"))
    return jax.shard_map(
        on_device, mesh=mesh, in_specs=placed, out_specs=(P("dp", "seq"), P(), P()), check_vma=False
    )
```

profile of v0, /device:TPU:0, one launch (start us, length us, event | category | flops | bytes accessed | tf_op | source)
XLA Modules:
  0.0 201.0 jit_solution(13949442704553326158)
XLA Ops:
  7.2 0.0 copy-start
  7.2 0.0 copy-start.2
  7.2 0.0 all-reduce.3.cloned.1.call-start
  7.2 0.7 convert_element_type.17
  8.0 0.9 fusion.17
  8.9 42.0 %all-reduce = (f32[64]{0:T(128)S(1)}, f32[64]{0:T(128)S(1)}, f32[64]{0:T(128)S(1)}) all-reduce(f32[64]{0:T(128)S(1)} %get-tuple-element.4, f32[64]{0:T(128)S(1)} %get-tuple-element.3, f32[64]{0:T(128)S(1)} %get-tuple-element.5), channel_id=1, replica_groups=mesh['dp'=8,'seq'=4] {'dp','seq'}, use_global_device_ids=true, to_apply=%region_5.0 | all-reduce | flops 192 | bytes 1536 | tf_op jit(solution)/shard_map/psum | solution.py:19
  50.9 0.0 copy-start.1
  50.9 1.0 select_reduce_fusion.2
  51.9 0.0 copy-done
  51.9 0.0 copy-start.3
  51.9 6.3 %fusion.13 = f32[1024]{0:T(1024)S(1)} fusion(bf16[4096,64]{0,1:T(8,128)(2,1)S(1)} %copy-done, bf16[1,1024,4096]{2,1,0:T(8,128)(2,1)} %param.6, f32[64]{0:T(128)} %param.8, s32[1024]{0:T(1024)} %bitcast.22), kind=kOutput, calls=%fused_computation.7 | convolution fusion | flops 537132032 | bytes 8921344 | tf_op jit(solution)/shard_map/dot_general | solution.py:15
  58.2 0.0 copy-done.2
  58.2 0.0 copy-done.1
  58.3 2.5 %fusion.4 = f32[4096,64]{0,1:T(8,128)} fusion(bf16[1,1024,4096]{2,1,0:T(8,128)(2,1)S(1)} %copy-done.1, f32[1024]{0:T(1024)S(1)} %multiply_multiply_fusion, s32[1024]{0:T(1024)S(1)} %bitcast.23), kind=kOutput, calls=%fused_computation.4 | convolution fusion | flops 537001984 | bytes 9445376 | tf_op jit(solution)/shard_map/dot_general | solution.py:29
  60.8 0.0 copy-done.3
  60.8 0.0 all-reduce.3.cloned.1.call-update
  60.8 0.1 select_reduce_fusion
  61.0 40.3 %psum.39 = f32[64]{0:T(128)} all-reduce(f32[64]{0:T(128)S(1)} %select_reduce_fusion), channel_id=1, replica_groups=mesh['dp'=8,'seq'=4] {'dp','seq'}, use_global_device_ids=true, to_apply=%region_10.11 | all-reduce | flops 64 | bytes 512 | tf_op jit(solution)/shard_map/psum | solution.py:36
  101.3 90.6 %all-reduce.3.cloned.1.call-done = f32[4096,64]{0,1:T(8,128)} async-done(((f32[4096,64]{0,1:T(8,128)}), f32[4096,64]{0,1:T(8,128)}) %all-reduce.3.cloned.1.call-update) | async-done | bytes 1048592 | tf_op jit(solution)/shard_map/psum | solution.py:36
  191.9 2.3 %copy.10 = f32[4096,64]{0,1:T(8,128)} copy(f32[4096,64]{0,1:T(8,128)} %all-reduce.3.cloned.1.call-done) | data formatting | bytes 2097152
  (2 shorter events, 0.0 us)
Async XLA Ops:
  7.2 44.8 %copy-start = (bf16[4096,64]{0,1:T(8,128)(2,1)S(1)}, bf16[4096,64]{0,1:T(8,128)(2,1)}, u32[]{:S(2)}) copy-start(bf16[4096,64]{0,1:T(8,128)(2,1)} %param.7) | copy-start | bytes 1572868
  7.2 51.1 %copy-start.2 = (s32[1,1024]{1,0:T(1,128)S(1)}, s32[1,1024]{1,0:T(1,128)}, u32[]{:S(2)}) copy-start(s32[1,1024]{1,0:T(1,128)} %param.10) | copy-start | bytes 12292
  7.2 184.7 %all-reduce.3.cloned.1.call-start = ((), (), s32[]{:S(2)}) async-start(), calls=%async_computation | async-start | bytes 2097152 | tf_op jit(solution)/shard_map/psum | solution.py:36
  50.9 7.3 %copy-start.1 = (bf16[1,1024,4096]{2,1,0:T(8,128)(2,1)S(1)}, bf16[1,1024,4096]{2,1,0:T(8,128)(2,1)}, u32[]{:S(2)}) copy-start(bf16[1,1024,4096]{2,1,0:T(8,128)(2,1)} %param.6) | copy-start | bytes 25165828
  51.9 8.9 %copy-start.3 = (f32[1024]{0:T(1024)}, f32[1024]{0:T(1024)S(1)}, u32[]{:S(2)}) copy-start(f32[1024]{0:T(1024)S(1)} %select_reduce_fusion.2) | copy-start | bytes 12292
Sparse Core Ops, SparseCore 0:
  60.9 130.8 all-reduce.2
where the time goes:
time: 202 us; the launch traced here: 201 us
  waiting for transfers between devices  90.6 us (45%)
  blocking collectives  82.4 us (41%)
  between operations  14.1 us (7%)
  matrix products  8.82 us (4%)
  other arithmetic  2.77 us (1%)
  local copies, waits for them, and re-layouts  2.3 us (1%)
    psum x1, waiting for transfers between devices, on_device(): weight_grad, bias_grad = lax.psum((weight_grad, bias_grad), ('dp', 'seq'))  90.6 us
    psum x1, blocking collectives, on_device(): counts, summed, squares = lax.psum((counts, summed, squares), ('dp', 'seq'))  42 us
    psum x1, blocking collectives, on_device(): weight_grad, bias_grad = lax.psum((weight_grad, bias_grad), ('dp', 'seq'))  40.3 us
    dot_general x1, matrix products, on_device(): scores = jnp.dot(states, value_weight, preferred_element_type=jnp.float32)  6.27 us
  transfers between devices with their start and end apart: 1, of which 1 were waited for; matrix products, arithmetic and copies ran while one was open for 0% of the time, Pallas kernels for 0%

commit v1 on v0

--- a/solution.py
+++ b/solution.py
@@ -33,7 +33,7 @@
         preferred_element_type=jnp.float32,
     )
     bias_grad = jnp.sum(coefficient, axis=0)
-    weight_grad, bias_grad = lax.psum((weight_grad, bias_grad), ("dp", "seq"))
+    weight_grad, bias_grad = lax.psum(lax.psum((weight_grad, bias_grad), "dp"), "seq")
     return (targets.reshape(returns.shape), weight_grad, bias_grad)
 
 

time: 202 us -> 187 us (0.926)
  blocking collectives: 82.4 us -> 68.2 us
    psum x1 -> x2, blocking collectives: 40.3 us -> 26.2 us  [the longest x1 20 us: on_device(): lax.psum((weight_grad, bias_grad), 'dp')]
    psum x1 -> x2, waiting for transfers between devices: 90.6 us -> 90 us  [the longest x1 78 us: on_device(): lax.psum((weight_grad, bias_grad), 'dp')]
  transfers between devices with their start and end apart: 1 -> 2, of which waited for: 1 -> 2; matrix products, arithmetic and copies ran while one was open for 0% -> 0% of each run, Pallas kernels for 0% -> 0%
where the time goes in v1:
time: 187 us; the launch traced here: 186 us
  waiting for transfers between devices  90 us (48%)
  blocking collectives  68.2 us (36%)
  between operations  14.1 us (8%)
  matrix products  8.82 us (5%)
  other arithmetic  2.77 us (1%)
  local copies, waits for them, and re-layouts  2.3 us (1%)
    psum x1, waiting for transfers between devices, on_device(): lax.psum((weight_grad, bias_grad), 'dp')  78 us
    psum x1, blocking collectives, on_device(): counts, summed, squares = lax.psum((counts, summed, squares), ('dp', 'seq'))  42 us
    psum x1, blocking collectives, on_device(): lax.psum((weight_grad, bias_grad), 'dp')  20 us
    psum x1, waiting for transfers between devices, on_device(): lax.psum(lax.psum((weight_grad, bias_grad), 'dp'), 'seq')  12 us
    dot_general x1, matrix products, on_device(): scores = jnp.dot(states, value_weight, preferred_element_type=jnp.float32)  6.27 us
    psum x1, blocking collectives, on_device(): lax.psum(lax.psum((weight_grad, bias_grad), 'dp'), 'seq')  6.15 us
  transfers between devices with their start and end apart: 2, of which 2 were waited for; matrix products, arithmetic and copies ran while one was open for 0% of the time, Pallas kernels for 0%

profile of v1, /device:TPU:0, one launch (start us, length us, event | category | flops | bytes accessed | tf_op | source)
XLA Modules:
  0.0 186.3 jit_solution(14436269642975887312)
XLA Ops:
  7.2 0.0 copy-start
  7.2 0.0 copy-start.2
  7.2 0.0 all-reduce.4.cloned.1.call-start
  7.2 0.7 convert_element_type.17
  8.0 0.9 fusion.17
  8.9 42.0 %all-reduce = (f32[64]{0:T(128)S(1)}, f32[64]{0:T(128)S(1)}, f32[64]{0:T(128)S(1)}) all-reduce(f32[64]{0:T(128)S(1)} %get-tuple-element.4, f32[64]{0:T(128)S(1)} %get-tuple-element.3, f32[64]{0:T(128)S(1)} %get-tuple-element.5), channel_id=1, replica_groups=mesh['dp'=8,'seq'=4] {'dp','seq'}, use_global_device_ids=true, to_apply=%region_5.0 | all-reduce | flops 192 | bytes 1536 | tf_op jit(solution)/shard_map/psum | solution.py:19
  50.9 0.0 copy-start.1
  50.9 1.0 select_reduce_fusion.2
  51.9 0.0 copy-done
  51.9 0.0 copy-start.3
  51.9 6.3 %fusion.13 = f32[1024]{0:T(1024)S(1)} fusion(bf16[4096,64]{0,1:T(8,128)(2,1)S(1)} %copy-done, bf16[1,1024,4096]{2,1,0:T(8,128)(2,1)} %param.6, f32[64]{0:T(128)} %param.8, s32[1024]{0:T(1024)} %bitcast.22), kind=kOutput, calls=%fused_computation.7 | convolution fusion | flops 537132032 | bytes 8921344 | tf_op jit(solution)/shard_map/dot_general | solution.py:15
  58.2 0.0 copy-done.2
  58.2 0.0 copy-done.1
  58.3 2.5 %fusion.4 = f32[4096,64]{0,1:T(8,128)} fusion(bf16[1,1024,4096]{2,1,0:T(8,128)(2,1)S(1)} %copy-done.1, f32[1024]{0:T(1024)S(1)} %multiply_multiply_fusion, s32[1024]{0:T(1024)S(1)} %bitcast.23), kind=kOutput, calls=%fused_computation.4 | convolution fusion | flops 537001984 | bytes 9445376 | tf_op jit(solution)/shard_map/dot_general | solution.py:29
  60.8 0.0 copy-done.3
  60.8 0.0 all-reduce.4.cloned.1.call-update
  60.8 0.0 all-reduce.6.cloned.1.call-start
  60.9 78.0 %all-reduce.4.cloned.1.call-done = f32[4096,64]{0,1:T(8,128)} async-done(((f32[4096,64]{0,1:T(8,128)}), f32[4096,64]{0,1:T(8,128)}) %all-reduce.4.cloned.1.call-update) | async-done | bytes 1048592 | tf_op jit(solution)/shard_map/psum | solution.py:36
  138.9 0.0 all-reduce.6.cloned.1.call-update
  138.9 0.1 select_reduce_fusion
  139.1 20.0 %psum.54 = f32[64]{0:T(128)S(1)} all-reduce(f32[64]{0:T(128)S(1)} %select_reduce_fusion), channel_id=1, replica_groups=mesh['dp'=8,'seq'=4] {'dp'}, use_global_device_ids=true, to_apply=%region_11.12 | all-reduce | flops 64 | bytes 512 | tf_op jit(solution)/shard_map/psum | solution.py:36
  159.1 6.2 %psum.55 = f32[64]{0:T(128)} all-reduce(f32[64]{0:T(128)S(1)} %psum.54), channel_id=1, replica_groups=mesh['dp'=8,'seq'=4] {'seq'}, use_global_device_ids=true, to_apply=%region_12.13 | all-reduce | flops 64 | bytes 512 | tf_op jit(solution)/shard_map/psum | solution.py:36
  165.3 12.0 %all-reduce.6.cloned.1.call-done = f32[4096,64]{0,1:T(8,128)} async-done(((f32[4096,64]{0,1:T(8,128)}), f32[4096,64]{0,1:T(8,128)}) %all-reduce.6.cloned.1.call-update) | async-done | bytes 1048592 | tf_op jit(solution)/shard_map/psum | solution.py:36
  177.2 2.3 %copy.11 = f32[4096,64]{0,1:T(8,128)} copy(f32[4096,64]{0,1:T(8,128)} %all-reduce.6.cloned.1.call-done) | data formatting | bytes 2097152
  (2 shorter events, 0.0 us)
Async XLA Ops:
  7.2 44.8 %copy-start = (bf16[4096,64]{0,1:T(8,128)(2,1)S(1)}, bf16[4096,64]{0,1:T(8,128)(2,1)}, u32[]{:S(2)}) copy-start(bf16[4096,64]{0,1:T(8,128)(2,1)} %param.7) | copy-start | bytes 1572868
  7.2 51.1 %copy-start.2 = (s32[1,1024]{1,0:T(1,128)S(1)}, s32[1,1024]{1,0:T(1,128)}, u32[]{:S(2)}) copy-start(s32[1,1024]{1,0:T(1,128)} %param.10) | copy-start | bytes 12292
  7.2 131.7 %all-reduce.4.cloned.1.call-start = ((), (), s32[]{:S(2)}) async-start(), calls=%async_computation | async-start | bytes 2097152 | tf_op jit(solution)/shard_map/psum | solution.py:36
  50.9 7.3 %copy-start.1 = (bf16[1,1024,4096]{2,1,0:T(8,128)(2,1)S(1)}, bf16[1,1024,4096]{2,1,0:T(8,128)(2,1)}, u32[]{:S(2)}) copy-start(bf16[1,1024,4096]{2,1,0:T(8,128)(2,1)} %param.6) | copy-start | bytes 25165828
  51.9 8.9 %copy-start.3 = (f32[1024]{0:T(1024)}, f32[1024]{0:T(1024)S(1)}, u32[]{:S(2)}) copy-start(f32[1024]{0:T(1024)S(1)} %select_reduce_fusion.2) | copy-start | bytes 12292
  60.8 116.4 %all-reduce.6.cloned.1.call-start = ((), (), s32[]{:S(2)}) async-start(), calls=%async_computation.1 | async-start | bytes 2097152 | tf_op jit(solution)/shard_map/psum | solution.py:36
Sparse Core Ops, SparseCore 0:
  60.9 77.9 all-reduce.3
  141.3 35.8 all-reduce.5
